TPU v7x, 128 devices: a whole 4x4x4 slice. The times are simulated.
128 devices in a mesh: dp: 4 (over x), fsdp: 32 (over z, y, core).
Axes of the slice: x: 4, y: 4, z: 4, core: 2. Of those that a mesh axis runs over, the one named last changes fastest.
Arguments:
- gradient: bfloat16 [4, 4096, 8, 1024], P('dp', 'fsdp'), may hold values from -3 to 3
- block_owner_index: int32 [32], replicated, may hold values from 0 to 31, as said below
- block_grid_cell: int32 [32], replicated, may hold values from 0 to 31, each once
- left_eigen_basis: float32 [64, 1024, 1024], P('fsdp', None, 'dp'), may hold values from -0.1875 to 0.1875
- right_eigen_basis: float32 [64, 1024, 1024], P('fsdp', None, 'dp'), may hold values from -0.1875 to 0.1875
- left_statistic_matrix: float32 [64, 1024, 1024], P('fsdp', None, 'dp'), may hold values from -6 to 6
- right_statistic_matrix: float32 [64, 1024, 1024], P('fsdp', None, 'dp'), may hold values from -6 to 6
- first_adam_moment: float32 [64, 1024, 1024], P('fsdp', None, 'dp'), may hold values from -0.09 to 0.09
- second_adam_moment: float32 [64, 1024, 1024], P('fsdp', None, 'dp'), may hold values from 1e-05 to 0.001
Outputs:
- new_left_stat: float32 [64, 1024, 1024], P('fsdp', None, 'dp')
- new_right_stat: float32 [64, 1024, 1024], P('fsdp', None, 'dp')
- new_first: float32 [64, 1024, 1024], P('fsdp', None, 'dp')
- new_second: float32 [64, 1024, 1024], P('fsdp', None, 'dp')
- update: bfloat16 [4096, 8, 1024], P('fsdp', None, 'dp')
Inputs may be any that keep to these rules, and one draw needn't show every extreme that they name: `block_owner_index`: no fsdp index owns more than 2 blocks; a quarter of the fsdp indices own 2 blocks and a quarter own none.
All inputs are finite; a program needn't handle non-finite values.
Results may differ from a plain program's by a relative error of at most 0.013.
Values may be sent and summed in bfloat16 or wider, within the bound.
No kernel may reach another device: no remote copies, remote signals or barrier semaphores. Data moves between devices by JAX's collectives and lax.ppermute only.
A program may use at most 128 MiB of HBM per device.

v0:
```python
import jax
import jax.numpy as jnp
from jax import lax
from jax.sharding import PartitionSpec as P


def in_order(blocks, dim):
    blocks = jnp.moveaxis(blocks, 0, dim)
    dims = blocks.shape
    return blocks.reshape(*dims[:dim], dims[dim] * dims[dim + 1], *dims[dim + 2 :])


def on_gathered_pieces(array, axis, dim, work, out_dim):
    width = array.shape[dim]
    pieces = jnp.split(array, 2, axis=dim) if width % 2 == 0 else [array]
    initial = jnp.arange(lax.axis_size(axis)) * width
    blocks = [lax.all_gather(piece, axis) for piece in pieces]
    made = [jax.vmap(work)(b, initial + k * (width // len(pieces))) for k, b in enumerate(blocks)]
    return in_order(jnp.concatenate(made, axis=out_dim + 1), out_dim)


def slot_lookup_table(block_owner_index, block_grid_cell, slot_count, per_owner):
    block_ids = jnp.arange(block_owner_index.shape[0], dtype=jnp.int32)
    shared = (block_owner_index[:, None] == block_owner_index[None, :]) & (
        block_ids[None, :] < block_ids[:, None]
    )
    rank_in = jnp.sum(shared.astype(jnp.int32), axis=1)
    block_slot_index = block_owner_index * per_owner + rank_in
    slot_ids = jnp.arange(slot_count, dtype=jnp.int32)
    matches = (block_slot_index[None, :] == slot_ids[:, None]).astype(jnp.int32)
    filled_marker = jnp.sum(matches, axis=1)
    slot_grid_cell = jnp.sum(matches * block_grid_cell[None, :], axis=1)
    return (block_slot_index, filled_marker, slot_grid_cell)


def local(
    gradient,
    block_owner_index,
    block_grid_cell,
    left_eigen_basis,
    right_eigen_basis,
    left_statistic_matrix,
    right_statistic_matrix,
    first_adam_moment,
    second_adam_moment,
):
    replicas = lax.axis_size("dp")
    members = lax.axis_size("fsdp")
    member = lax.axis_index("fsdp")
    column_group = lax.axis_index("dp")
    per_owner = left_eigen_basis.shape[0]
    block = left_eigen_basis.shape[1]
    width = left_eigen_basis.shape[2]
    band_rows = gradient.shape[1]
    grid_cols = gradient.shape[2]
    bands = block // band_rows
    grid_rows = members // bands
    piece_rows = band_rows // members
    slot_count = per_owner * members
    partial_terms = gradient.reshape(band_rows, grid_cols, replicas, width).astype(jnp.float32)
    reduced = lax.psum_scatter(
        partial_terms.astype(jnp.bfloat16), "dp", scatter_dimension=2, tiled=True
    ).astype(jnp.float32)
    reduced = reduced.reshape(band_rows, grid_cols, width).astype(jnp.bfloat16)
    block_slot_index, filled_marker, slot_grid_cell = slot_lookup_table(
        block_owner_index, block_grid_cell, slot_count, per_owner
    )
    my_filled = lax.dynamic_slice_in_dim(filled_marker, member * per_owner, per_owner, 0)
    split_band = reduced.reshape(members, piece_rows, grid_cols, width)
    received = lax.all_to_all(split_band, "fsdp", split_axis=0, concat_axis=0, tiled=True)
    by_cell = received.reshape(grid_rows, bands, piece_rows, grid_cols, width)
    by_cell = jnp.transpose(by_cell, (0, 3, 1, 2, 4)).reshape(
        grid_rows * grid_cols, bands, piece_rows, width
    )
    leaving = jnp.take(by_cell, slot_grid_cell, axis=0)
    leaving = jnp.where((filled_marker > 0)[:, None, None, None], leaving, jnp.zeros_like(leaving))
    leaving = leaving.reshape(members, per_owner, bands, piece_rows, width)
    landed = lax.all_to_all(leaving, "fsdp", split_axis=0, concat_axis=0, tiled=True)
    col_piece = jnp.transpose(landed, (1, 2, 0, 3, 4)).reshape(per_owner, block, width)
    gathered = lax.all_gather(col_piece, "dp", axis=2, tiled=True)
    row_piece = lax.dynamic_slice_in_dim(gathered, column_group * width, width, 1)
    new_left = 0.95 * left_statistic_matrix + 0.05 * jnp.einsum(
        "sik,sjk->sij", gathered, row_piece, preferred_element_type=jnp.float32
    )
    new_right = 0.95 * right_statistic_matrix + 0.05 * jnp.einsum(
        "ski,skj->sij", gathered, col_piece, preferred_element_type=jnp.float32
    )
    half_turn = jnp.einsum("sik,sij->skj", left_eigen_basis, gathered.astype(jnp.float32)).astype(
        jnp.bfloat16
    )

    def turn_rows(piece, start):
        return jnp.einsum("skj,sjc->skc", piece.astype(jnp.float32), right_eigen_basis)

    turned = on_gathered_pieces(half_turn, "dp", 1, turn_rows, 1)
    new_first = 0.9 * first_adam_moment + 0.1 * turned
    new_second = 0.999 * second_adam_moment + 0.001 * turned * turned
    direction = new_first / (jnp.sqrt(new_second) + 1e-08)
    full_left = lax.all_gather(left_eigen_basis, "dp", axis=2, tiled=True)
    applied = jnp.einsum("sik,skc->sic", full_left, direction)
    piece = right_eigen_basis
    moved = lax.psum_scatter(
        jnp.einsum("sic,sjc->jsi", applied, piece), "dp", scatter_dimension=0, tiled=True
    )
    backward = jnp.transpose(moved.astype(jnp.bfloat16), (1, 2, 0))
    parted = backward.reshape(per_owner, bands, members, piece_rows, width)
    parted = jnp.transpose(parted, (2, 0, 1, 3, 4))
    parted = jnp.where((my_filled > 0)[None, :, None, None, None], parted, jnp.zeros_like(parted))
    homed = lax.all_to_all(parted, "fsdp", split_axis=0, concat_axis=0, tiled=True)
    homed = homed.reshape(slot_count, bands, piece_rows, width)
    all_cells = jnp.arange(grid_rows * grid_cols, dtype=jnp.int32)
    all_hits = (block_grid_cell[None, :] == all_cells[:, None]).astype(jnp.int32)
    cell_slot = jnp.sum(all_hits * block_slot_index[None, :], axis=1)
    per_cell = jnp.take(homed, cell_slot, axis=0).reshape(
        grid_rows, grid_cols, bands, piece_rows, width
    )
    per_cell = jnp.transpose(per_cell, (0, 2, 3, 1, 4)).reshape(
        members, piece_rows, grid_cols, width
    )
    update = lax.all_to_all(per_cell, "fsdp", split_axis=0, concat_axis=0, tiled=True).reshape(
        band_rows, grid_cols, width
    )
    return (new_left, new_right, new_first, new_second, update)


def solution(mesh):
    in_specs = (
        P("dp", "fsdp", None, None),
        P(),
        P(),
        P("fsdp", None, "dp"),
        P("fsdp", None, "dp"),
        P("fsdp", None, "dp"),
        P("fsdp", None, "dp"),
        P("fsdp", None, "dp"),
        P("fsdp", None, "dp"),
    )
    out_specs = (
        P("fsdp", None, "dp"),
        P("fsdp", None, "dp"),
        P("fsdp", None, "dp"),
        P("fsdp", None, "dp"),
        P("fsdp", None, "dp"),
    )
    return jax.shard_map(local, mesh=mesh, in_specs=in_specs, out_specs=out_specs, check_vma=False)
```

profile of v0, /device:TPU:1, one launch (start us, length us, event | category | flops | bytes accessed | tf_op | source)
XLA Modules:
  0.0 404.2 jit_solution(3661794692890048232)
XLA Ops:
  7.2 0.0 copy-start
  7.2 0.0 reduce-scatter.3.cloned.1.call-start
  7.2 3.2 copy.61
  10.4 0.0 reduce-scatter.3.cloned.1.call-update
  10.4 0.6 copy-done.6
  11.1 0.2 convert_reduce_fusion.1
  11.3 0.1 convert_reduce_fusion
  11.4 0.1 reduce_sum.47
  11.5 0.1 gt.22
  11.6 32.2 %reduce-scatter.3.cloned.1.call-done = bf16[128,8,1,256]{3,1,0,2:T(8,128)(2,1)} async-done(((bf16[128,8,4,256]{3,1,0,2:T(8,128)(2,1)}), bf16[128,8,1,256]{3,1,0,2:T(8,128)(2,1)}) %reduce-scatter.3.cloned.1.call-update) | async-done | bytes 524304 | tf_op jit(solution)/shard_map/reduce_scatter | solution.py:61
  43.8 7.8 %all-to-all-start = ((bf16[32,4,8,256]{3,2,1,0:T(8,128)(2,1)}), bf16[32,4,8,256]{3,2,1,0:T(8,128)(2,1)S(1)}, u32[]{:S(2)}, u32[]{:S(2)}) async-start(bf16[32,4,8,256]{3,2,1,0:T(8,128)(2,1)} %bitcast.89), calls=%async_computation.1 | async-start | bytes 1048576 | tf_op jit(solution)/shard_map/all_to_all | solution.py:70
  51.6 0.0 all-gather.7.cloned.1.call-start
  51.7 11.3 %all-to-all-done = bf16[32,4,8,256]{3,2,1,0:T(8,128)(2,1)S(1)} async-done(((bf16[32,4,8,256]{3,2,1,0:T(8,128)(2,1)}), bf16[32,4,8,256]{3,2,1,0:T(8,128)(2,1)S(1)}, u32[]{:S(2)}, u32[]{:S(2)}) %all-to-all-start) | async-done | bytes 524320 | tf_op jit(solution)/shard_map/all_to_all | solution.py:70
  63.0 0.3 copy.62
  63.3 1.6 gather_fusion
  64.9 1.4 select_select_fusion
  66.3 20.7 %all_to_all.20 = bf16[32,2,8,4,256]{4,2,3,1,0:T(8,128)(2,1)S(1)} all-to-all(bf16[32,2,8,4,256]{4,2,3,1,0:T(8,128)(2,1)S(1)} %select_select_fusion), channel_id=1, replica_groups=mesh['dp'=4,'fsdp'=32] {'fsdp'}, dimensions={0} | all-to-all | bytes 2097152 | tf_op jit(solution)/shard_map/all_to_all | solution.py:78
  87.0 0.5 copy.63
  87.5 1.1 reshape.101
  88.6 0.0 all-gather.7.cloned.1.call-update
  88.6 0.0 all-gather.13.cloned.1.call-start
  88.7 46.0 %all-gather.7.cloned.1.call-done = bf16[2,1024,1024]{2,1,0:T(8,128)(2,1)} async-done(((bf16[2,1024,256]{2,1,0:T(8,128)(2,1)}), bf16[2,1024,1024]{2,1,0:T(8,128)(2,1)}) %all-gather.7.cloned.1.call-update) | async-done | bytes 4194320 | tf_op jit(solution)/shard_map/all_gather | solution.py:80
  134.7 4.6 %fusion.16 = bf16[2,256,1024]{1,2,0:T(8,128)(2,1)S(1)} fusion(bf16[2,1024,1024]{2,1,0:T(8,128)(2,1)} %all-gather.7.cloned.1.call-done, f32[2,1024,256]{2,1,0:T(8,128)} %param.12), kind=kOutput, calls=%fused_computation.21 | convolution fusion | flops 1073741824 | bytes 7340032 | tf_op jit(solution)/shard_map/sik,sij->skj/dot_general | solution.py:88
  139.3 0.2 fusion.39
  139.5 1.0 copy.68
  140.5 0.0 all-gather.13.cloned.1.call-update
  140.5 0.0 all-gather.11.cloned.1.call-start
  140.6 1.0 copy.66
  141.6 0.0 all-gather.11.cloned.1.call-update
  141.6 0.0 all-gather.9.cloned.1.call-start
  141.6 2.7 convert.4
  144.3 0.0 all-gather.9.cloned.1.call-update
  144.3 0.0 reduce-scatter.5.cloned.1.call-start
  144.4 29.2 %all-gather.13.cloned.1.call-done = bf16[8,128,1024]{2,1,0:T(8,128)(2,1)} async-done(((bf16[2,128,1024]{2,1,0:T(8,128)(2,1)}), bf16[8,128,1024]{2,1,0:T(8,128)(2,1)}) %all-gather.13.cloned.1.call-update) | async-done | bytes 2097168 | tf_op jit(solution)/shard_map/all_gather | solution.py:17
  173.6 2.3 fusion.22
  175.9 30.6 %all-gather.11.cloned.1.call-done = bf16[8,128,1024]{2,1,0:T(8,128)(2,1)} async-done(((bf16[2,128,1024]{2,1,0:T(8,128)(2,1)}), bf16[8,128,1024]{2,1,0:T(8,128)(2,1)}) %all-gather.11.cloned.1.call-update) | async-done | bytes 2097168 | tf_op jit(solution)/shard_map/all_gather | solution.py:17
  206.5 2.3 fusion.17
  208.8 0.0 copy-start.3
  208.8 0.0 copy-start.4
  208.8 0.1 pad_maximum_fusion
  208.9 1.4 copy-done.3
  210.4 0.6 copy-done.4
  211.0 2.6 fusion
  213.6 45.1 %all-gather.9.cloned.1.call-done = bf16[2,1024,1024]{2,1,0:T(8,128)(2,1)} async-done(((bf16[2,1024,256]{2,1,0:T(8,128)(2,1)}), bf16[2,1024,1024]{2,1,0:T(8,128)(2,1)}) %all-gather.9.cloned.1.call-update) | async-done | bytes 4194320 | tf_op jit(solution)/shard_map/all_gather | solution.py:99
  258.7 9.2 %convolution_bitcast_fusion = f32[1024,2,1024]{0,2,1:T(8,128)} fusion(f32[2,1024,256]{2,1,0:T(8,128)S(1)} %copy-done, bf16[2,1024,1024]{2,1,0:T(8,128)(2,1)} %all-gather.9.cloned.1.call-done, f32[2,1024,256]{2,1,0:T(8,128)} %get-tuple-element.18, f32[2,1024,256]{2,1,0:T(8,128)} %get-tuple-element.19), kind=kOutput, calls=%fused_computation.2 | convolution fusion | flops 2148532224 | bytes 18874368 | tf_op jit(solution)/shard_map/sic,sjc->jsi/dot_general | solution.py:103
  267.9 0.0 reduce-scatter.5.cloned.1.call-update
  268.0 0.1 select_reduce_fusion
  268.1 0.1 reduce_sum.50
  268.2 0.1 dynamic-slice_compare_fusion
  268.2 82.6 %reduce-scatter.5.cloned.1.call-done = f32[256,2,1024]{0,2,1:T(8,128)} async-done(((f32[1024,2,1024]{0,2,1:T(8,128)}), f32[256,2,1024]{0,2,1:T(8,128)}) %reduce-scatter.5.cloned.1.call-update) | async-done | bytes 2097168 | tf_op jit(solution)/shard_map/reduce_scatter | solution.py:102
  350.9 1.7 convert_bitcast_fusion
  352.6 0.3 reshape.103
  352.9 0.0 copy-start.2
  352.9 1.6 fusion.27
  354.5 7.8 %all-to-all-start.2 = ((bf16[32,2,8,4,256]{4,2,3,1,0:T(8,128)(2,1)}), bf16[32,2,8,4,256]{4,2,3,1,0:T(8,128)(2,1)S(1)}, u32[]{:S(2)}, u32[]{:S(2)}) async-start(bf16[32,2,8,4,256]{4,2,3,1,0:T(8,128)(2,1)} %fusion.27), calls=%async_computation.4 | async-start | bytes 2097152 | tf_op jit(solution)/shard_map/all_to_all | solution.py:109
  362.3 5.9 %multiply_add_fusion = f32[2,1024,256]{2,1,0:T(8,128)} fusion(f32[2,1024,256]{2,1,0:T(8,128)} %param.15, bf16[2,1024,1024]{2,1,0:T(8,128)(2,1)} %all-gather.7.cloned.1.call-done, bf16[2,1024,256]{2,1,0:T(8,128)(2,1)S(1)} %copy-done.2), kind=kOutput, calls=%fused_computation.18 | convolution fusion | flops 1075314688 | bytes 9437184 | tf_op jit(solution)/shard_map/ski,skj->sij/dot_general | solution.py:85
  368.2 11.1 %all-to-all-done.2 = bf16[32,2,8,4,256]{4,2,3,1,0:T(8,128)(2,1)S(1)} async-done(((bf16[32,2,8,4,256]{4,2,3,1,0:T(8,128)(2,1)}), bf16[32,2,8,4,256]{4,2,3,1,0:T(8,128)(2,1)S(1)}, u32[]{:S(2)}, u32[]{:S(2)}) %all-to-all-start.2) | async-done | bytes 1048608 | tf_op jit(solution)/shard_map/all_to_all | solution.py:109
  379.3 0.6 gather_fusion.1
  379.9 0.1 select_bitcast_fusion
  380.0 1.1 copy.73
  381.1 3.9 all-to-all-start.3
  385.0 6.0 %multiply_add_fusion.1 = f32[2,1024,256]{2,1,0:T(8,128)} fusion(f32[2,1024,256]{2,1,0:T(8,128)} %param.14, bf16[2,1024,1024]{2,1,0:T(8,128)(2,1)} %all-gather.7.cloned.1.call-done, s32[]{:T(128)S(6)} %select_n.66), kind=kOutput, calls=%fused_computation.19 | convolution fusion | flops 1075314688 | bytes 9437188 | tf_op jit(solution)/shard_map/sik,sjk->sij/dot_general | solution.py:82
  391.0 5.5 %all-to-all-done.3 = bf16[32,4,8,256]{3,2,1,0:T(8,128)(2,1)S(1)} async-done(((bf16[32,4,8,256]{3,2,1,0:T(8,128)(2,1)}), bf16[32,4,8,256]{3,2,1,0:T(8,128)(2,1)S(1)}, u32[]{:S(2)}, u32[]{:S(2)}) %all-to-all-start.3) | async-done | bytes 524320 | tf_op jit(solution)/shard_map/all_to_all | solution.py:120
  396.6 0.8 copy.91
  (15 shorter events, 0.1 us)
Async XLA Ops:
  7.2 166.4 %copy-start = (f32[2,1024,256]{2,1,0:T(8,128)S(1)}, f32[2,1024,256]{2,1,0:T(8,128)}, u32[]{:S(2)}) copy-start(f32[2,1024,256]{2,1,0:T(8,128)} %param.13) | copy-start | bytes 6291460
  7.2 36.6 %reduce-scatter.3.cloned.1.call-start = ((), (), s32[]{:S(2)}) async-start(), calls=%async_computation.6 | async-start | bytes 2621440 | tf_op jit(solution)/shard_map/reduce_scatter | solution.py:61
  10.4 0.7 copy-start.6
  10.4 0.8 copy-start.5
  43.8 19.2 %all-to-all-start = ((bf16[32,4,8,256]{3,2,1,0:T(8,128)(2,1)}), bf16[32,4,8,256]{3,2,1,0:T(8,128)(2,1)S(1)}, u32[]{:S(2)}, u32[]{:S(2)}) async-start(bf16[32,4,8,256]{3,2,1,0:T(8,128)(2,1)} %bitcast.89), calls=%async_computation.1 | async-start | bytes 1048576 | tf_op jit(solution)/shard_map/all_to_all | solution.py:70
  51.6 83.1 %all-gather.7.cloned.1.call-start = ((), (), s32[]{:S(2)}) async-start(), calls=%async_computation.7 | async-start | bytes 5242880 | tf_op jit(solution)/shard_map/all_gather | solution.py:80
  88.6 84.9 %all-gather.13.cloned.1.call-start = ((), (), s32[]{:S(2)}) async-start(), calls=%async_computation.11 | async-start | bytes 2621440 | tf_op jit(solution)/shard_map/all_gather | solution.py:17
  140.5 66.0 %all-gather.11.cloned.1.call-start = ((), (), s32[]{:S(2)}) async-start(), calls=%async_computation.10 | async-start | bytes 2621440 | tf_op jit(solution)/shard_map/all_gather | solution.py:17
  141.6 117.2 %all-gather.9.cloned.1.call-start = ((), (), s32[]{:S(2)}) async-start(), calls=%async_computation.8 | async-start | bytes 5242880 | tf_op jit(solution)/shard_map/all_gather | solution.py:99
  144.3 206.5 %reduce-scatter.5.cloned.1.call-start = ((), (), s32[]{:S(2)}) async-start(), calls=%async_computation.9 | async-start | bytes 10485760 | tf_op jit(solution)/shard_map/reduce_scatter | solution.py:102
  208.8 1.6 copy-start.3
  208.8 2.2 copy-start.4
  352.9 9.4 %copy-start.2 = (bf16[2,1024,256]{2,1,0:T(8,128)(2,1)S(1)}, bf16[2,1024,256]{2,1,0:T(8,128)(2,1)}, u32[]{:S(2)}) copy-start(bf16[2,1024,256]{2,1,0:T(8,128)(2,1)} %reshape.101) | copy-start | bytes 3145732
  354.5 24.8 %all-to-all-start.2 = ((bf16[32,2,8,4,256]{4,2,3,1,0:T(8,128)(2,1)}), bf16[32,2,8,4,256]{4,2,3,1,0:T(8,128)(2,1)S(1)}, u32[]{:S(2)}, u32[]{:S(2)}) async-start(bf16[32,2,8,4,256]{4,2,3,1,0:T(8,128)(2,1)} %fusion.27), calls=%async_computation.4 | async-start | bytes 2097152 | tf_op jit(solution)/shard_map/all_to_all | solution.py:109
  381.1 15.5 %all-to-all-start.3 = ((bf16[32,4,8,256]{3,2,1,0:T(8,128)(2,1)}), bf16[32,4,8,256]{3,2,1,0:T(8,128)(2,1)S(1)}, u32[]{:S(2)}, u32[]{:S(2)}) async-start(bf16[32,4,8,256]{3,2,1,0:T(8,128)(2,1)} %bitcast.28), calls=%async_computation.5 | async-start | bytes 1048576 | tf_op jit(solution)/shard_map/all_to_all | solution.py:120
  385.0 12.3 %copy-start.1 = (f32[2,1024,256]{2,1,0:T(8,128)S(1)}, f32[2,1024,256]{2,1,0:T(8,128)}, u32[]{:S(2)}) copy-start(f32[2,1024,256]{2,1,0:T(8,128)} %param.13) | copy-start | bytes 6291460
Sparse Core Ops, SparseCore 0:
  11.0 32.7 reduce-scatter.2
  88.8 45.8 all-gather.6
  140.6 32.8 all-gather.12
  175.6 30.7 all-gather.10
  208.5 50.1 all-gather.8
  268.1 82.7 reduce-scatter.4
where the time goes:
time: 405 us; the launch traced here: 404 us
  waiting for transfers between devices  294 us (73%)
  matrix products  30.3 us (7%)
  blocking collectives  20.7 us (5%)
  starting transfers between devices  19.7 us (5%)
  local copies, waits for them, and re-layouts  14.6 us (4%)
  between operations  14.3 us (4%)
  other arithmetic  10.8 us (3%)
    reduce_scatter x1, waiting for transfers between devices, local(): lax.psum_scatter(jnp.einsum('sic,sjc->jsi', applied, piece), 'dp', scatte...  82.6 us
    all_gather x2, waiting for transfers between devices, on_gathered_pieces(): blocks = [lax.all_gather(piece, axis) for piece in pieces]  59.8 us
    all_gather x1, waiting for transfers between devices, local(): gathered = lax.all_gather(col_piece, 'dp', axis=2, tiled=True)  46 us
    all_gather x1, waiting for transfers between devices, local(): full_left = lax.all_gather(left_eigen_basis, 'dp', axis=2, tiled=True)  45.1 us
    reduce_scatter x1, waiting for transfers between devices, local(): lax.psum_scatter(partial_terms.astype(jnp.bfloat16), 'dp', scatter_dimens...  32.2 us
    all_to_all x1, blocking collectives, local(): lax.all_to_all(leaving, 'fsdp', split_axis=0, concat_axis=0, tiled=True)  20.7 us
    all_to_all x1, waiting for transfers between devices, local(): lax.all_to_all(split_band, 'fsdp', split_axis=0, concat_axis=0, tiled=True)  11.3 us
    all_to_all x1, waiting for transfers between devices, local(): lax.all_to_all(parted, 'fsdp', split_axis=0, concat_axis=0, tiled=True)  11.1 us
  transfers between devices with their start and end apart: 9, of which 9 were waited for; matrix products, arithmetic and copies ran while one was open for 6% of the time, Pallas kernels for 0%

commit v1 on v0

--- a/solution.py
+++ b/solution.py
@@ -96,7 +96,7 @@
     new_first = 0.9 * first_adam_moment + 0.1 * turned
     new_second = 0.999 * second_adam_moment + 0.001 * turned * turned
     direction = new_first / (jnp.sqrt(new_second) + 1e-08)
-    full_left = lax.all_gather(left_eigen_basis, "dp", axis=2, tiled=True)
+    full_left = jnp.concatenate(lax.all_gather(left_eigen_basis, "dp"), axis=2)
     applied = jnp.einsum("sik,skc->sic", full_left, direction)
     piece = right_eigen_basis
     moved = lax.psum_scatter(

time: 405 us -> 405 us (level)
  waiting for transfers between devices: 294 us -> 287 us
  local copies, waits for them, and re-layouts: 14.6 us -> 20.9 us
    reshape x0 -> x1, local copies, waits for them, and re-layouts: none -> 6.29 us  [local(): full_left = jnp.concatenate(lax.all_gather(left_eigen_basis, 'dp'), axis=2)]
  transfers between devices with their start and end apart: 9 -> 9, of which waited for: 9 -> 9; matrix products, arithmetic and copies ran while one was open for 6% -> 8% of each run, Pallas kernels for 0% -> 0%
where the time goes in v1:
time: 405 us; the launch traced here: 404 us
  waiting for transfers between devices  287 us (71%)
  matrix products  30.6 us (8%)
  local copies, waits for them, and re-layouts  20.9 us (5%)
  blocking collectives  20.7 us (5%)
  starting transfers between devices  19.7 us (5%)
  between operations  14.3 us (4%)
  other arithmetic  10.8 us (3%)
    reduce_scatter x1, waiting for transfers between devices, local(): lax.psum_scatter(jnp.einsum('sic,sjc->jsi', applied, piece), 'dp', scatte...  80.5 us
    all_gather x2, waiting for transfers between devices, on_gathered_pieces(): blocks = [lax.all_gather(piece, axis) for piece in pieces]  57.5 us
    all_gather x1, waiting for transfers between devices, local(): full_left = jnp.concatenate(lax.all_gather(left_eigen_basis, 'dp'), axis=2)  45.6 us
    all_gather x1, waiting for transfers between devices, local(): gathered = lax.all_gather(col_piece, 'dp', axis=2, tiled=True)  43.2 us
    reduce_scatter x1, waiting for transfers between devices, local(): lax.psum_scatter(partial_terms.astype(jnp.bfloat16), 'dp', scatter_dimens...  32.2 us
    all_to_all x1, blocking collectives, local(): lax.all_to_all(leaving, 'fsdp', split_axis=0, concat_axis=0, tiled=True)  20.7 us
    all_to_all x1, waiting for transfers between devices, local(): lax.all_to_all(split_band, 'fsdp', split_axis=0, concat_axis=0, tiled=True)  11.3 us
    all_to_all x1, waiting for transfers between devices, local(): lax.all_to_all(parted, 'fsdp', split_axis=0, concat_axis=0, tiled=True)  11.1 us
  transfers between devices with their start and end apart: 9, of which 9 were waited for; matrix products, arithmetic and copies ran while one was open for 8% of the time, Pallas kernels for 0%

profile of v1, /device:TPU:1, one launch (start us, length us, event | category | flops | bytes accessed | tf_op | source)
XLA Modules:
  0.0 404.1 jit_solution(12529445119142255741)
XLA Ops:
  7.2 0.0 copy-start
  7.2 0.0 reduce-scatter.3.cloned.1.call-start
  7.2 3.2 copy.67
  10.4 0.0 reduce-scatter.3.cloned.1.call-update
  10.4 0.6 copy-done.6
  11.1 0.2 convert_reduce_fusion.1
  11.3 0.1 convert_reduce_fusion
  11.4 0.1 reduce_sum.47
  11.5 0.1 gt.22
  11.6 32.2 %reduce-scatter.3.cloned.1.call-done = bf16[128,8,1,256]{3,1,0,2:T(8,128)(2,1)} async-done(((bf16[128,8,4,256]{3,1,0,2:T(8,128)(2,1)}), bf16[128,8,1,256]{3,1,0,2:T(8,128)(2,1)}) %reduce-scatter.3.cloned.1.call-update) | async-done | bytes 524304 | tf_op jit(solution)/shard_map/reduce_scatter | solution.py:61
  43.8 7.8 %all-to-all-start = ((bf16[32,4,8,256]{3,2,1,0:T(8,128)(2,1)}), bf16[32,4,8,256]{3,2,1,0:T(8,128)(2,1)S(1)}, u32[]{:S(2)}, u32[]{:S(2)}) async-start(bf16[32,4,8,256]{3,2,1,0:T(8,128)(2,1)} %bitcast.95), calls=%async_computation.1 | async-start | bytes 1048576 | tf_op jit(solution)/shard_map/all_to_all | solution.py:70
  51.6 0.0 all-gather.8.cloned.1.call-start
  51.7 11.3 %all-to-all-done = bf16[32,4,8,256]{3,2,1,0:T(8,128)(2,1)S(1)} async-done(((bf16[32,4,8,256]{3,2,1,0:T(8,128)(2,1)}), bf16[32,4,8,256]{3,2,1,0:T(8,128)(2,1)S(1)}, u32[]{:S(2)}, u32[]{:S(2)}) %all-to-all-start) | async-done | bytes 524320 | tf_op jit(solution)/shard_map/all_to_all | solution.py:70
  63.0 0.3 copy.68
  63.3 1.6 gather_fusion
  64.9 1.4 select_select_fusion
  66.3 20.7 %all_to_all.20 = bf16[32,2,8,4,256]{4,2,3,1,0:T(8,128)(2,1)S(1)} all-to-all(bf16[32,2,8,4,256]{4,2,3,1,0:T(8,128)(2,1)S(1)} %select_select_fusion), channel_id=1, replica_groups=mesh['dp'=4,'fsdp'=32] {'fsdp'}, dimensions={0} | all-to-all | bytes 2097152 | tf_op jit(solution)/shard_map/all_to_all | solution.py:78
  87.0 0.5 copy.69
  87.5 1.1 reshape.107
  88.6 0.0 all-gather.8.cloned.1.call-update
  88.6 0.0 all-gather.14.cloned.1.call-start
  88.7 2.7 convert.4
  91.4 0.0 all-gather.14.cloned.1.call-update
  91.4 0.0 all-gather.12.cloned.1.call-start
  91.4 43.2 %all-gather.8.cloned.1.call-done = bf16[2,1024,1024]{2,1,0:T(8,128)(2,1)} async-done(((bf16[2,1024,256]{2,1,0:T(8,128)(2,1)}), bf16[2,1024,1024]{2,1,0:T(8,128)(2,1)}) %all-gather.8.cloned.1.call-update) | async-done | bytes 4194320 | tf_op jit(solution)/shard_map/all_gather | solution.py:80
  134.7 4.6 %fusion.16 = bf16[2,256,1024]{1,2,0:T(8,128)(2,1)S(1)} fusion(bf16[2,1024,1024]{2,1,0:T(8,128)(2,1)} %all-gather.8.cloned.1.call-done, f32[2,1024,256]{2,1,0:T(8,128)} %param.12), kind=kOutput, calls=%fused_computation.21 | convolution fusion | flops 1073741824 | bytes 7340032 | tf_op jit(solution)/shard_map/sik,sij->skj/dot_general | solution.py:88
  139.3 0.2 fusion.39
  139.5 1.0 copy.74
  140.5 0.0 all-gather.12.cloned.1.call-update
  140.5 0.0 all-gather.10.cloned.1.call-start
  140.6 1.0 copy.72
  141.6 0.0 all-gather.10.cloned.1.call-update
  141.6 0.0 reduce-scatter.5.cloned.1.call-start
  141.6 45.6 %all-gather.14.cloned.1.call-done = bf16[8,1024,256]{2,1,0:T(8,128)(2,1)} async-done(((bf16[2,1024,256]{2,1,0:T(8,128)(2,1)}), bf16[8,1024,256]{2,1,0:T(8,128)(2,1)}) %all-gather.14.cloned.1.call-update) | async-done | bytes 4194320 | tf_op jit(solution)/shard_map/all_gather | solution.py:99
  187.3 6.3 %copy.76 = bf16[2,1024,4,256]{1,3,2,0:T(8,128)(2,1)} copy(bf16[2,1024,4,256]{3,1,0,2:T(8,128)(2,1)} %bitcast.86) | data formatting | bytes 8388608 | tf_op jit(solution)/shard_map/reshape | solution.py:99
  193.6 26.9 %all-gather.12.cloned.1.call-done = bf16[8,128,1024]{2,1,0:T(8,128)(2,1)} async-done(((bf16[2,128,1024]{2,1,0:T(8,128)(2,1)}), bf16[8,128,1024]{2,1,0:T(8,128)(2,1)}) %all-gather.12.cloned.1.call-update) | async-done | bytes 2097168 | tf_op jit(solution)/shard_map/all_gather | solution.py:17
  220.5 2.3 fusion.22
  222.8 30.6 %all-gather.10.cloned.1.call-done = bf16[8,128,1024]{2,1,0:T(8,128)(2,1)} async-done(((bf16[2,128,1024]{2,1,0:T(8,128)(2,1)}), bf16[8,128,1024]{2,1,0:T(8,128)(2,1)}) %all-gather.10.cloned.1.call-update) | async-done | bytes 2097168 | tf_op jit(solution)/shard_map/all_gather | solution.py:17
  253.4 2.3 fusion.17
  255.7 0.0 copy-start.3
  255.7 0.0 copy-start.4
  255.7 0.1 pad_maximum_fusion
  255.9 1.4 copy-done.3
  257.3 0.6 copy-done.4
  257.9 2.6 fusion
  260.6 9.4 %convolution_bitcast_fusion = f32[1024,2,1024]{0,2,1:T(8,128)} fusion(f32[2,1024,256]{2,1,0:T(8,128)S(1)} %copy-done, bf16[2,1024,1024]{1,2,0:T(8,128)(2,1)} %bitcast.83, f32[2,1024,256]{2,1,0:T(8,128)} %get-tuple-element.18, f32[2,1024,256]{2,1,0:T(8,128)} %get-tuple-element.19), kind=kOutput, calls=%fused_computation.2 | convolution fusion | flops 2148532224 | bytes 18874368 | tf_op jit(solution)/shard_map/sic,sjc->jsi/dot_general | solution.py:103
  270.0 0.0 reduce-scatter.5.cloned.1.call-update
  270.0 0.1 select_reduce_fusion
  270.1 0.1 reduce_sum.50
  270.2 0.1 dynamic-slice_compare_fusion
  270.3 80.5 %reduce-scatter.5.cloned.1.call-done = f32[256,2,1024]{0,2,1:T(8,128)} async-done(((f32[1024,2,1024]{0,2,1:T(8,128)}), f32[256,2,1024]{0,2,1:T(8,128)}) %reduce-scatter.5.cloned.1.call-update) | async-done | bytes 2097168 | tf_op jit(solution)/shard_map/reduce_scatter | solution.py:102
  350.8 1.7 convert_bitcast_fusion
  352.5 0.3 reshape.111
  352.8 1.6 fusion.27
  354.4 7.8 %all-to-all-start.2 = ((bf16[32,2,8,4,256]{4,2,3,1,0:T(8,128)(2,1)}), bf16[32,2,8,4,256]{4,2,3,1,0:T(8,128)(2,1)S(1)}, u32[]{:S(2)}, u32[]{:S(2)}) async-start(bf16[32,2,8,4,256]{4,2,3,1,0:T(8,128)(2,1)} %fusion.27), calls=%async_computation.4 | async-start | bytes 2097152 | tf_op jit(solution)/shard_map/all_to_all | solution.py:109
  362.2 5.9 %multiply_add_fusion = f32[2,1024,256]{2,1,0:T(8,128)} fusion(f32[2,1024,256]{2,1,0:T(8,128)} %param.15, bf16[2,1024,1024]{2,1,0:T(8,128)(2,1)} %all-gather.8.cloned.1.call-done, bf16[2,1024,256]{2,1,0:T(8,128)(2,1)S(1)} %copy-done.2), kind=kOutput, calls=%fused_computation.18 | convolution fusion | flops 1075314688 | bytes 9437184 | tf_op jit(solution)/shard_map/ski,skj->sij/dot_general | solution.py:85
  368.1 11.1 %all-to-all-done.2 = bf16[32,2,8,4,256]{4,2,3,1,0:T(8,128)(2,1)S(1)} async-done(((bf16[32,2,8,4,256]{4,2,3,1,0:T(8,128)(2,1)}), bf16[32,2,8,4,256]{4,2,3,1,0:T(8,128)(2,1)S(1)}, u32[]{:S(2)}, u32[]{:S(2)}) %all-to-all-start.2) | async-done | bytes 1048608 | tf_op jit(solution)/shard_map/all_to_all | solution.py:109
  379.2 0.6 gather_fusion.1
  379.8 0.1 select_bitcast_fusion
  379.9 1.1 copy.81
  381.0 3.9 all-to-all-start.3
  385.0 6.0 %multiply_add_fusion.1 = f32[2,1024,256]{2,1,0:T(8,128)} fusion(f32[2,1024,256]{2,1,0:T(8,128)} %param.14, bf16[2,1024,1024]{2,1,0:T(8,128)(2,1)} %all-gather.8.cloned.1.call-done, s32[]{:T(128)S(6)} %select_n.66), kind=kOutput, calls=%fused_computation.19 | convolution fusion | flops 1075314688 | bytes 9437188 | tf_op jit(solution)/shard_map/sik,sjk->sij/dot_general | solution.py:82
  391.0 5.5 %all-to-all-done.3 = bf16[32,4,8,256]{3,2,1,0:T(8,128)(2,1)S(1)} async-done(((bf16[32,4,8,256]{3,2,1,0:T(8,128)(2,1)}), bf16[32,4,8,256]{3,2,1,0:T(8,128)(2,1)S(1)}, u32[]{:S(2)}, u32[]{:S(2)}) %all-to-all-start.3) | async-done | bytes 524320 | tf_op jit(solution)/shard_map/all_to_all | solution.py:120
  396.5 0.8 copy.100
  (16 shorter events, 0.1 us)
Async XLA Ops:
  7.2 213.3 %copy-start = (f32[2,1024,256]{2,1,0:T(8,128)S(1)}, f32[2,1024,256]{2,1,0:T(8,128)}, u32[]{:S(2)}) copy-start(f32[2,1024,256]{2,1,0:T(8,128)} %param.13) | copy-start | bytes 6291460
  7.2 36.6 %reduce-scatter.3.cloned.1.call-start = ((), (), s32[]{:S(2)}) async-start(), calls=%async_computation.6 | async-start | bytes 2621440 | tf_op jit(solution)/shard_map/reduce_scatter | solution.py:61
  10.4 0.7 copy-start.6
  10.4 0.8 copy-start.5
  43.8 19.2 %all-to-all-start = ((bf16[32,4,8,256]{3,2,1,0:T(8,128)(2,1)}), bf16[32,4,8,256]{3,2,1,0:T(8,128)(2,1)S(1)}, u32[]{:S(2)}, u32[]{:S(2)}) async-start(bf16[32,4,8,256]{3,2,1,0:T(8,128)(2,1)} %bitcast.95), calls=%async_computation.1 | async-start | bytes 1048576 | tf_op jit(solution)/shard_map/all_to_all | solution.py:70
  51.6 83.1 %all-gather.8.cloned.1.call-start = ((), (), s32[]{:S(2)}) async-start(), calls=%async_computation.7 | async-start | bytes 5242880 | tf_op jit(solution)/shard_map/all_gather | solution.py:80
  88.6 98.6 %all-gather.14.cloned.1.call-start = ((), (), s32[]{:S(2)}) async-start(), calls=%async_computation.11 | async-start | bytes 5242880 | tf_op jit(solution)/shard_map/all_gather | solution.py:99
  91.4 129.1 %all-gather.12.cloned.1.call-start = ((), (), s32[]{:S(2)}) async-start(), calls=%async_computation.10 | async-start | bytes 2621440 | tf_op jit(solution)/shard_map/all_gather | solution.py:17
  140.5 112.9 %all-gather.10.cloned.1.call-start = ((), (), s32[]{:S(2)}) async-start(), calls=%async_computation.9 | async-start | bytes 2621440 | tf_op jit(solution)/shard_map/all_gather | solution.py:17
  141.6 209.2 %reduce-scatter.5.cloned.1.call-start = ((), (), s32[]{:S(2)}) async-start(), calls=%async_computation.8 | async-start | bytes 10485760 | tf_op jit(solution)/shard_map/reduce_scatter | solution.py:102
  255.7 1.6 copy-start.3
  255.7 2.2 copy-start.4
  352.8 9.4 %copy-start.2 = (bf16[2,1024,256]{2,1,0:T(8,128)(2,1)S(1)}, bf16[2,1024,256]{2,1,0:T(8,128)(2,1)}, u32[]{:S(2)}) copy-start(bf16[2,1024,256]{2,1,0:T(8,128)(2,1)} %reshape.107) | copy-start | bytes 3145732
  354.4 24.8 %all-to-all-start.2 = ((bf16[32,2,8,4,256]{4,2,3,1,0:T(8,128)(2,1)}), bf16[32,2,8,4,256]{4,2,3,1,0:T(8,128)(2,1)S(1)}, u32[]{:S(2)}, u32[]{:S(2)}) async-start(bf16[32,2,8,4,256]{4,2,3,1,0:T(8,128)(2,1)} %fusion.27), calls=%async_computation.4 | async-start | bytes 2097152 | tf_op jit(solution)/shard_map/all_to_all | solution.py:109
  381.0 15.5 %all-to-all-start.3 = ((bf16[32,4,8,256]{3,2,1,0:T(8,128)(2,1)}), bf16[32,4,8,256]{3,2,1,0:T(8,128)(2,1)S(1)}, u32[]{:S(2)}, u32[]{:S(2)}) async-start(bf16[32,4,8,256]{3,2,1,0:T(8,128)(2,1)} %bitcast.31), calls=%async_computation.5 | async-start | bytes 1048576 | tf_op jit(solution)/shard_map/all_to_all | solution.py:120
  385.0 12.3 %copy-start.1 = (f32[2,1024,256]{2,1,0:T(8,128)S(1)}, f32[2,1024,256]{2,1,0:T(8,128)}, u32[]{:S(2)}) copy-start(f32[2,1024,256]{2,1,0:T(8,128)} %param.13) | copy-start | bytes 6291460
Sparse Core Ops, SparseCore 0:
  11.0 32.7 reduce-scatter.2
  88.8 45.8 all-gather.7
  136.9 50.3 all-gather.13
  189.4 31.0 all-gather.11
  222.6 30.7 all-gather.9
  270.1 80.6 reduce-scatter.4
